TPU v7x, 256 devices: a whole 4x4x8 slice. The times are simulated.
256 devices in a mesh: batch: 4 (over x), proto: 64 (over y, z, core).
Axes of the slice: x: 4, y: 4, z: 8, core: 2. Of those that a mesh axis runs over, the one named last changes fastest.
Arguments:
- view_codes: bfloat16 [4096, 1024], P('batch', 'proto'), may hold values from -80 to 80
- predictor_view_embeddings: bfloat16 [4096, 1024], P('batch', 'proto'), may hold values from -80 to 80
- prototypes: bfloat16 [65536, 1024], P('proto'), may hold values from -64 to 64
Outputs:
- assignments: bfloat16 [4096, 65536], P('batch', 'proto')
- loss_rows: float32 [4096], P('batch')
All inputs are finite; a program needn't handle non-finite values.
Results may differ from a plain program's by a relative error of at most 0.0034.
Values may be sent and summed in bfloat16 or wider, within the bound.
A program may use at most 64 MiB of HBM per device.

v0:
```python
import jax
import jax.numpy as jnp
from jax import lax
from jax.sharding import PartitionSpec as P

SINK_ITERS = 3
EPSILON = 0.05
SOFTMAX_TEMP_VALUE = 0.1


def copy_for_each(shard, axis):
    copies = jnp.broadcast_to(shard, (lax.axis_size(axis), *shard.shape))
    return lax.all_to_all(copies, axis, split_axis=0, concat_axis=0, tiled=True)


def of_everyone(shard, axis):
    return copy_for_each(shard, axis).sum(axis=0)


def together(arrays, axis):
    ravelled, at, gathered = (jnp.concatenate([a.reshape(-1) for a in arrays]), 0, [])
    subtotal = of_everyone(ravelled, axis)
    for a in arrays:
        gathered.append(subtotal[at : at + a.size].reshape(a.shape))
        at += a.size
    return tuple(gathered)


def normalized(prototypes):
    weights = prototypes.astype(jnp.float32)
    return (weights * lax.rsqrt(jnp.sum(weights * weights, axis=1, keepdims=True) + 1e-06)).astype(
        jnp.bfloat16
    )


def view_scores(embedded, unit_prototype_rows):
    products = jnp.dot(embedded, unit_prototype_rows.T, preferred_element_type=jnp.float32)
    values = embedded.astype(jnp.float32)
    inverse_factor = lax.rsqrt(jnp.sum(values * values, axis=1) + 1e-06)
    return products * inverse_factor[:, None]


def local(view_codes, predictor_view_embeddings, prototypes):
    unit_prototype_rows = normalized(prototypes)
    whole_first, whole_second = (
        lax.all_gather(view_codes, "proto", axis=1, tiled=True),
        lax.all_gather(predictor_view_embeddings, "proto", axis=1, tiled=True),
    )
    scores_codes = view_scores(whole_first, unit_prototype_rows)
    predictor_scores = view_scores(whole_second, unit_prototype_rows)
    kernel = jnp.exp(scores_codes / EPSILON)
    rows_total = kernel.shape[0] * lax.axis_size("batch")
    protos_total = kernel.shape[1] * lax.axis_size("proto")
    logit_scores = predictor_scores / SOFTMAX_TEMP_VALUE
    scale_rows = jnp.ones((kernel.shape[0],), jnp.float32)
    for iteration in range(SINK_ITERS):
        col_part = jnp.dot(scale_rows, kernel, precision=lax.Precision.HIGHEST)
        col_sums = of_everyone(col_part, "batch")
        scale_cols = 1.0 / (protos_total * col_sums)
        row_part = jnp.dot(kernel, scale_cols, precision=lax.Precision.HIGHEST)
        row_sums = of_everyone(row_part, "proto")
        scale_rows = 1.0 / (rows_total * row_sums)
    assign = kernel * scale_cols[None, :] * (rows_total * scale_rows)[:, None]
    assignments = (protos_total * assign).astype(jnp.bfloat16)
    cross_part = jnp.sum(assign * logit_scores, axis=1)
    totals, cross_term = together((jnp.sum(jnp.exp(logit_scores), axis=1), cross_part), "proto")
    loss_rows = jnp.log(totals) - cross_term
    return (assignments, loss_rows)


def solution(mesh):
    placed = (P("batch", "proto"), P("batch", "proto"), P("proto", None))
    return jax.shard_map(
        local,
        mesh=mesh,
        in_specs=placed,
        out_specs=(P("batch", "proto"), P("batch")),
        check_vma=False,
    )
```

profile of v0, /device:TPU:1, one launch (start us, length us, event | category | flops | bytes accessed | tf_op | source)
XLA Modules:
  0.0 249.5 jit_solution(1705991306893637967)
XLA Ops:
  7.2 0.0 copy-start.1
  7.2 0.0 all-gather.3.cloned.1.call-start
  7.2 0.7 all-gather.3.cloned.1.call-update
  7.9 0.0 all-gather.5.cloned.1.call-start
  8.0 0.7 all-gather.5.cloned.1.call-update
  8.7 2.1 fusion
  10.7 81.8 %all-gather.3.cloned.1.call-done = bf16[1024,1024]{0,1:T(8,128)(2,1)} async-done(((bf16[1024,16]{0,1:T(8,128)(2,1)}), bf16[1024,1024]{0,1:T(8,128)(2,1)}) %all-gather.3.cloned.1.call-update) | async-done | bytes 2097168 | tf_op jit(solution)/shard_map/all_gather | solution.py:46
  92.6 2.1 multiply_reduce_fusion.1
  94.6 0.0 copy-done.1
  94.7 4.0 %multiply_exponential_fusion = f32[1024,1024]{1,0:T(8,128)S(1)} fusion(bf16[1024,1024]{0,1:T(8,128)(2,1)} %all-gather.3.cloned.1.call-done, f32[1024]{0:T(1024)S(1)} %add_rsqrt_fusion.1, bf16[1024,1024]{1,0:T(8,128)(2,1)S(1)} %copy-done.1, f32[1024]{0:T(1024)S(1)} %add_rsqrt_fusion.2), kind=kOutput, calls=%fused_computation.25 | convolution fusion | flops 2152726528 | bytes 8396800 | tf_op jit(solution)/shard_map/dot_general | solution.py:37
  98.6 0.0 copy-start
  98.7 1.9 copy-done
  100.6 3.6 %fusion.14 = f32[1,1024]{1,0:T(1,128)S(1)} fusion(f32[1024,1024]{1,0:T(8,128)S(1)} %multiply_exponential_fusion), kind=kOutput, calls=%fused_computation.19 | convolution fusion | flops 12582912 | bytes 4198400 | tf_op jit(solution)/shard_map/dot_general | solution.py:57
  104.2 8.1 %all_to_all.42 = f32[4,1,1024]{2,1,0:T(1,128)S(1)} all-to-all(f32[4,1,1024]{2,1,0:T(1,128)S(1)} %broadcast_in_dim.26), channel_id=1, replica_groups=mesh['batch'=4,'proto'=64] {'batch'}, dimensions={0} | all-to-all | bytes 32768 | tf_op jit(solution)/shard_map/all_to_all | solution.py:13
  112.2 4.4 %fusion.12 = f32[1,1024]{1,0:T(1,128)S(1)} fusion(f32[1024,1]{0,1:T(1,128)S(1)} %bitcast.52, f32[1024,1024]{1,0:T(8,128)} %copy-done), kind=kOutput, calls=%fused_computation.17 | convolution fusion | flops 12582912 | bytes 4202496 | tf_op jit(solution)/shard_map/dot_general | solution.py:60
  116.7 0.1 broadcast_in_dim.27
  116.8 19.7 %all_to_all.43 = f32[64,1,1024]{2,1,0:T(1,128)S(1)} all-to-all(f32[64,1,1024]{2,1,0:T(1,128)S(1)} %broadcast_in_dim.27), channel_id=1, replica_groups=mesh['batch'=4,'proto'=64] {'proto'}, dimensions={0} | all-to-all | bytes 524288 | tf_op jit(solution)/shard_map/all_to_all | solution.py:13
  136.5 0.2 reduce_sum.111
  136.7 5.6 %fusion.10 = f32[1,1024]{1,0:T(1,128)S(1)} fusion(f32[1024,1]{0,1:T(1,128)S(1)} %bitcast.53, f32[1024,1024]{1,0:T(8,128)} %copy-done), kind=kOutput, calls=%fused_computation.15 | convolution fusion | flops 12582912 | bytes 4202496 | tf_op jit(solution)/shard_map/dot_general | solution.py:57
  142.4 6.6 %all_to_all.44 = f32[4,1,1024]{2,1,0:T(1,128)S(1)} all-to-all(f32[4,1,1024]{2,1,0:T(1,128)S(1)} %broadcast_in_dim.28), channel_id=1, replica_groups=mesh['batch'=4,'proto'=64] {'batch'}, dimensions={0} | all-to-all | bytes 32768 | tf_op jit(solution)/shard_map/all_to_all | solution.py:13
  149.0 4.4 %fusion.8 = f32[1,1024]{1,0:T(1,128)S(1)} fusion(f32[1024,1]{0,1:T(1,128)S(1)} %bitcast.54, f32[1024,1024]{1,0:T(8,128)} %copy-done), kind=kOutput, calls=%fused_computation.13 | convolution fusion | flops 12582912 | bytes 4202496 | tf_op jit(solution)/shard_map/dot_general | solution.py:60
  153.4 0.1 broadcast_in_dim.29
  153.6 19.1 %all_to_all.45 = f32[64,1,1024]{2,1,0:T(1,128)S(1)} all-to-all(f32[64,1,1024]{2,1,0:T(1,128)S(1)} %broadcast_in_dim.29), channel_id=1, replica_groups=mesh['batch'=4,'proto'=64] {'proto'}, dimensions={0} | all-to-all | bytes 524288 | tf_op jit(solution)/shard_map/all_to_all | solution.py:13
  172.6 0.2 reduce_sum.113
  172.8 5.6 %fusion.6 = f32[1,1024]{1,0:T(1,128)S(1)} fusion(f32[1024,1]{0,1:T(1,128)S(1)} %bitcast.55, f32[1024,1024]{1,0:T(8,128)} %copy-done), kind=kOutput, calls=%fused_computation.11 | convolution fusion | flops 12582912 | bytes 4202496 | tf_op jit(solution)/shard_map/dot_general | solution.py:57
  178.5 6.6 %all_to_all.46 = f32[4,1,1024]{2,1,0:T(1,128)S(1)} all-to-all(f32[4,1,1024]{2,1,0:T(1,128)S(1)} %broadcast_in_dim.30), channel_id=1, replica_groups=mesh['batch'=4,'proto'=64] {'batch'}, dimensions={0} | all-to-all | bytes 32768 | tf_op jit(solution)/shard_map/all_to_all | solution.py:13
  185.1 4.4 %fusion.4 = f32[1,1024]{1,0:T(1,128)S(1)} fusion(f32[1024,1]{0,1:T(1,128)S(1)} %bitcast.51, f32[1024,1024]{1,0:T(8,128)} %copy-done), kind=kOutput, calls=%fused_computation.8 | convolution fusion | flops 12582912 | bytes 4202496 | tf_op jit(solution)/shard_map/dot_general | solution.py:60
  189.5 0.8 broadcast_in_dim.31
  190.4 7.9 %all-to-all-start.5 = ((f32[64,1,1024]{2,1,0:T(1,128)}), f32[64,1,1024]{2,1,0:T(1,128)S(1)}, u32[]{:S(2)}, u32[]{:S(2)}) async-start(f32[64,1,1024]{2,1,0:T(1,128)} %broadcast_in_dim.31), calls=%async_computation.5 | async-start | bytes 524288 | tf_op jit(solution)/shard_map/all_to_all | solution.py:13
  198.3 0.0 all-gather.5.cloned.1.call-done
  198.3 2.1 multiply_reduce_fusion
  200.4 9.9 %all-to-all-done.5 = f32[64,1,1024]{2,1,0:T(1,128)S(1)} async-done(((f32[64,1,1024]{2,1,0:T(1,128)}), f32[64,1,1024]{2,1,0:T(1,128)S(1)}, u32[]{:S(2)}, u32[]{:S(2)}) %all-to-all-start.5) | async-done | bytes 262176 | tf_op jit(solution)/shard_map/all_to_all | solution.py:13
  210.3 0.2 reduce_sum.115
  210.5 6.9 %fusion.2 = (f32[1024]{0:T(1024)S(1)}, f32[1024]{0:T(1024)S(1)}, bf16[1024,1024]{0,1:T(8,128)(2,1)}) fusion(f32[1024]{0:T(1024)S(1)} %add_rsqrt_fusion, f32[1024]{0:T(1024)S(1)} %divide_multiply_fusion, f32[1024]{0:T(1024)S(1)} %multiply_divide_fusion, f32[1024,1024]{1,0:T(8,128)} %copy-done, bf16[1024,1024]{0,1:T(8,128)(2,1)} %all-gather.5.cloned.1.call-done, ...), kind=kOutput, calls=%fused_computation.6 | convolution fusion | flops 2160064512 | bytes 10510336 | tf_op jit(solution)/shard_map/dot_general | solution.py:37
  217.3 1.1 broadcast_in_dim.32
  218.4 6.0 %all-to-all-start.6 = ((f32[64,1,2048]{2,1,0:T(1,128)}), f32[64,1,2048]{2,1,0:T(1,128)S(1)}, u32[]{:S(2)}, u32[]{:S(2)}) async-start(f32[64,1,2048]{2,1,0:T(1,128)} %broadcast_in_dim.32), calls=%async_computation.6 | async-start | bytes 1048576 | tf_op jit(solution)/shard_map/all_to_all | solution.py:13
  224.4 3.9 %copy.14 = bf16[1024,1024]{1,0:T(8,128)(2,1)} copy(bf16[1024,1024]{0,1:T(8,128)(2,1)} %get-tuple-element.10) | data formatting | bytes 4194304
  228.4 13.3 %all-to-all-done.6 = f32[64,1,2048]{2,1,0:T(1,128)S(1)} async-done(((f32[64,1,2048]{2,1,0:T(1,128)}), f32[64,1,2048]{2,1,0:T(1,128)S(1)}, u32[]{:S(2)}, u32[]{:S(2)}) %all-to-all-start.6) | async-done | bytes 524320 | tf_op jit(solution)/shard_map/all_to_all | solution.py:13
  241.7 0.3 reduce_sum.119
  242.0 0.6 slice_subtract_fusion
  (16 shorter events, 0.2 us)
Async XLA Ops:
  7.2 87.5 %copy-start.1 = (bf16[1024,1024]{1,0:T(8,128)(2,1)S(1)}, bf16[1024,1024]{1,0:T(8,128)(2,1)}, u32[]{:S(2)}) copy-start(bf16[1024,1024]{1,0:T(8,128)(2,1)} %param.5) | copy-start | bytes 6291460
  7.2 85.4 %all-gather.3.cloned.1.call-start = ((), (), s32[]{:S(2)}) async-start(), calls=%async_computation.7 | async-start | bytes 2129920 | tf_op jit(solution)/shard_map/all_gather | solution.py:46
  7.9 190.4 %all-gather.5.cloned.1.call-start = ((), (), s32[]{:S(2)}) async-start(), calls=%async_computation.8 | async-start | bytes 2129920 | tf_op jit(solution)/shard_map/all_gather | solution.py:47
  98.6 1.9 copy-start
  190.4 19.9 %all-to-all-start.5 = ((f32[64,1,1024]{2,1,0:T(1,128)}), f32[64,1,1024]{2,1,0:T(1,128)S(1)}, u32[]{:S(2)}, u32[]{:S(2)}) async-start(f32[64,1,1024]{2,1,0:T(1,128)} %broadcast_in_dim.31), calls=%async_computation.5 | async-start | bytes 524288 | tf_op jit(solution)/shard_map/all_to_all | solution.py:13
  218.4 23.3 %all-to-all-start.6 = ((f32[64,1,2048]{2,1,0:T(1,128)}), f32[64,1,2048]{2,1,0:T(1,128)S(1)}, u32[]{:S(2)}, u32[]{:S(2)}) async-start(f32[64,1,2048]{2,1,0:T(1,128)} %broadcast_in_dim.32), calls=%async_computation.6 | async-start | bytes 1048576 | tf_op jit(solution)/shard_map/all_to_all | solution.py:13
Sparse Core Ops, SparseCore 0:
  10.8 81.7 all-gather.2
  95.3 75.9 all-gather.4
where the time goes:
time: 250 us; the launch traced here: 249 us
  waiting for transfers between devices  106 us (42%)
  blocking collectives  59.9 us (24%)
  matrix products  39 us (16%)
  between operations  14.2 us (6%)
  starting transfers between devices  14 us (6%)
  local copies, waits for them, and re-layouts  8.12 us (3%)
  other arithmetic  7.8 us (3%)
    all_gather x1, waiting for transfers between devices, local(): lax.all_gather(view_codes, 'proto', axis=1, tiled=True)  81.8 us
    all_to_all x5, blocking collectives, copy_for_each(): return lax.all_to_all(copies, axis, split_axis=0, concat_axis=0, tiled=True)  59.9 us
    all_to_all x2, waiting for transfers between devices, copy_for_each(): return lax.all_to_all(copies, axis, split_axis=0, concat_axis=0, tiled=True)  23.2 us
    dot_general x3, matrix products, local(): col_part = jnp.dot(scale_rows, kernel, precision=lax.Precision.HIGHEST)  14.9 us
    all_to_all x2, starting transfers between devices, copy_for_each(): return lax.all_to_all(copies, axis, split_axis=0, concat_axis=0, tiled=True)  13.9 us
    dot_general x3, matrix products, local(): row_part = jnp.dot(kernel, scale_cols, precision=lax.Precision.HIGHEST)  13.3 us
    dot_general x2, matrix products, view_scores(): jnp.dot(embedded, unit_prototype_rows.T, preferred_element_type=jnp.float32)  10.9 us
    unnamed x5, local copies, waits for them, and re-layouts  5.86 us
  transfers between devices with their start and end apart: 4, of which 3 were waited for; matrix products, arithmetic and copies ran while one was open for 18% of the time, Pallas kernels for 0%

commit v1 on v0

--- a/solution.py
+++ b/solution.py
@@ -1,3 +1,4 @@
+import functools
 import jax
 import jax.numpy as jnp
 from jax import lax
@@ -6,6 +7,16 @@
 SINK_ITERS = 3
 EPSILON = 0.05
 SOFTMAX_TEMP_VALUE = 0.1
+
+
+def search_routes_all(tile_in, net_axis):
+    view_out = jnp.concatenate(
+        jax.lax.all_to_all(jnp.stack(jax.lax.psum(1, net_axis) * [tile_in]), net_axis, 0, 0), axis=1
+    )
+    return view_out
+
+
+point_the_lane = functools.partial(search_routes_all, net_axis="proto")
 
 
 def copy_for_each(shard, axis):
@@ -43,7 +54,7 @@
 def local(view_codes, predictor_view_embeddings, prototypes):
     unit_prototype_rows = normalized(prototypes)
     whole_first, whole_second = (
-        lax.all_gather(view_codes, "proto", axis=1, tiled=True),
+        point_the_lane(view_codes),
         lax.all_gather(predictor_view_embeddings, "proto", axis=1, tiled=True),
     )
     scores_codes = view_scores(whole_first, unit_prototype_rows)

time: 250 us -> 230 us (0.920)
  waiting for transfers between devices: 106 us -> 73.5 us
  starting transfers between devices: 14 us -> 26.6 us
    all_gather x1 -> x0, waiting for transfers between devices: 81.8 us -> none  [local(): lax.all_gather(view_codes, 'proto', axis=1, tiled=True)]
    all_to_all x0 -> x1, waiting for transfers between devices: none -> 49.6 us  [search_routes_all(): jax.lax.all_to_all(jnp.stack(jax.lax.psum(1, net_axis) * [tile_in]), net_...]
    all_to_all x0 -> x1, starting transfers between devices: none -> 13.1 us  [search_routes_all(): jax.lax.all_to_all(jnp.stack(jax.lax.psum(1, net_axis) * [tile_in]), net_...]
where the time goes in v1:
time: 230 us; the launch traced here: 229 us
  waiting for transfers between devices  73.5 us (32%)
  blocking collectives  59.3 us (26%)
  matrix products  39 us (17%)
  starting transfers between devices  26.6 us (12%)
  between operations  14.2 us (6%)
  local copies, waits for them, and re-layouts  10.5 us (5%)
  other arithmetic  6.21 us (3%)
    all_to_all x5, blocking collectives, copy_for_each(): return lax.all_to_all(copies, axis, split_axis=0, concat_axis=0, tiled=True)  59.3 us
    all_to_all x1, waiting for transfers between devices, search_routes_all(): jax.lax.all_to_all(jnp.stack(jax.lax.psum(1, net_axis) * [tile_in]), net_...  49.6 us
    all_to_all x2, waiting for transfers between devices, copy_for_each(): return lax.all_to_all(copies, axis, split_axis=0, concat_axis=0, tiled=True)  23.2 us
    dot_general x3, matrix products, local(): col_part = jnp.dot(scale_rows, kernel, precision=lax.Precision.HIGHEST)  14.9 us
    all_to_all x2, starting transfers between devices, copy_for_each(): return lax.all_to_all(copies, axis, split_axis=0, concat_axis=0, tiled=True)  13.4 us
    dot_general x3, matrix products, local(): row_part = jnp.dot(kernel, scale_cols, precision=lax.Precision.HIGHEST)  13.3 us
    all_to_all x1, starting transfers between devices, search_routes_all(): jax.lax.all_to_all(jnp.stack(jax.lax.psum(1, net_axis) * [tile_in]), net_...  13.1 us
    dot_general x2, matrix products, view_scores(): jnp.dot(embedded, unit_prototype_rows.T, preferred_element_type=jnp.float32)  10.9 us
  transfers between devices with their start and end apart: 4, of which 3 were waited for; matrix products, arithmetic and copies ran while one was open for 18% of the time, Pallas kernels for 0%

profile of v1, /device:TPU:1, one launch (start us, length us, event | category | flops | bytes accessed | tf_op | source)
XLA Modules:
  0.0 229.3 jit_solution(16280516851337928532)
XLA Ops:
  7.2 2.3 %stack.2 = bf16[64,1024,16]{1,2,0:T(8,128)(2,1)} broadcast(bf16[1024,16]{0,1:T(8,128)(2,1)} %param.3), dimensions={1,2} | broadcast | bytes 2129920 | tf_op jit(solution)/shard_map/stack | solution.py:14
  9.5 13.1 %all-to-all-start = ((bf16[64,1024,16]{1,2,0:T(8,128)(2,1)}), bf16[64,1024,16]{1,2,0:T(8,128)(2,1)S(1)}, u32[]{:S(2)}, u32[]{:S(2)}) async-start(bf16[64,1024,16]{1,2,0:T(8,128)(2,1)} %stack.2), calls=%async_computation | async-start | bytes 4194304 | tf_op jit(solution)/shard_map/all_to_all | solution.py:14
  22.7 0.0 all-gather.2.cloned.1.call-start
  22.7 0.7 all-gather.2.cloned.1.call-update
  23.4 2.1 fusion
  25.5 49.6 %all-to-all-done = bf16[64,1024,16]{1,2,0:T(8,128)(2,1)S(1)} async-done(((bf16[64,1024,16]{1,2,0:T(8,128)(2,1)}), bf16[64,1024,16]{1,2,0:T(8,128)(2,1)S(1)}, u32[]{:S(2)}, u32[]{:S(2)}) %all-to-all-start) | async-done | bytes 2097184 | tf_op jit(solution)/shard_map/all_to_all | solution.py:14
  75.1 0.5 multiply_reduce_fusion.1
  75.5 4.0 %multiply_exponential_fusion = f32[1024,1024]{1,0:T(8,128)S(1)} fusion(bf16[1024,1024]{0,1:T(8,128)(2,1)S(1)} %bitcast.49, f32[1024]{0:T(1024)S(1)} %add_rsqrt_fusion.1, bf16[1024,1024]{1,0:T(8,128)(2,1)} %param.5, f32[1024]{0:T(1024)S(1)} %add_rsqrt_fusion.2), kind=kOutput, calls=%fused_computation.25 | convolution fusion | flops 2152726528 | bytes 8396800 | tf_op jit(solution)/shard_map/dot_general | solution.py:48
  79.5 0.0 copy-start
  79.5 1.9 copy-done
  81.5 3.6 %fusion.14 = f32[1,1024]{1,0:T(1,128)S(1)} fusion(f32[1024,1024]{1,0:T(8,128)S(1)} %multiply_exponential_fusion), kind=kOutput, calls=%fused_computation.19 | convolution fusion | flops 12582912 | bytes 4198400 | tf_op jit(solution)/shard_map/dot_general | solution.py:68
  85.0 8.0 %all_to_all.47 = f32[4,1,1024]{2,1,0:T(1,128)S(1)} all-to-all(f32[4,1,1024]{2,1,0:T(1,128)S(1)} %broadcast_in_dim.26), channel_id=1, replica_groups=mesh['batch'=4,'proto'=64] {'batch'}, dimensions={0} | all-to-all | bytes 32768 | tf_op jit(solution)/shard_map/all_to_all | solution.py:24
  93.1 4.4 %fusion.12 = f32[1,1024]{1,0:T(1,128)S(1)} fusion(f32[1024,1]{0,1:T(1,128)S(1)} %bitcast.57, f32[1024,1024]{1,0:T(8,128)} %copy-done), kind=kOutput, calls=%fused_computation.17 | convolution fusion | flops 12582912 | bytes 4202496 | tf_op jit(solution)/shard_map/dot_general | solution.py:71
  97.5 0.1 broadcast_in_dim.27
  97.7 19.1 %all_to_all.48 = f32[64,1,1024]{2,1,0:T(1,128)S(1)} all-to-all(f32[64,1,1024]{2,1,0:T(1,128)S(1)} %broadcast_in_dim.27), channel_id=1, replica_groups=mesh['batch'=4,'proto'=64] {'proto'}, dimensions={0} | all-to-all | bytes 524288 | tf_op jit(solution)/shard_map/all_to_all | solution.py:24
  116.7 0.2 reduce_sum.111
  116.9 5.6 %fusion.10 = f32[1,1024]{1,0:T(1,128)S(1)} fusion(f32[1024,1]{0,1:T(1,128)S(1)} %bitcast.58, f32[1024,1024]{1,0:T(8,128)} %copy-done), kind=kOutput, calls=%fused_computation.15 | convolution fusion | flops 12582912 | bytes 4202496 | tf_op jit(solution)/shard_map/dot_general | solution.py:68
  122.6 6.6 %all_to_all.49 = f32[4,1,1024]{2,1,0:T(1,128)S(1)} all-to-all(f32[4,1,1024]{2,1,0:T(1,128)S(1)} %broadcast_in_dim.28), channel_id=1, replica_groups=mesh['batch'=4,'proto'=64] {'batch'}, dimensions={0} | all-to-all | bytes 32768 | tf_op jit(solution)/shard_map/all_to_all | solution.py:24
  129.2 4.4 %fusion.8 = f32[1,1024]{1,0:T(1,128)S(1)} fusion(f32[1024,1]{0,1:T(1,128)S(1)} %bitcast.59, f32[1024,1024]{1,0:T(8,128)} %copy-done), kind=kOutput, calls=%fused_computation.13 | convolution fusion | flops 12582912 | bytes 4202496 | tf_op jit(solution)/shard_map/dot_general | solution.py:71
  133.6 0.1 broadcast_in_dim.29
  133.8 19.0 %all_to_all.50 = f32[64,1,1024]{2,1,0:T(1,128)S(1)} all-to-all(f32[64,1,1024]{2,1,0:T(1,128)S(1)} %broadcast_in_dim.29), channel_id=1, replica_groups=mesh['batch'=4,'proto'=64] {'proto'}, dimensions={0} | all-to-all | bytes 524288 | tf_op jit(solution)/shard_map/all_to_all | solution.py:24
  152.7 0.2 reduce_sum.113
  152.9 5.6 %fusion.6 = f32[1,1024]{1,0:T(1,128)S(1)} fusion(f32[1024,1]{0,1:T(1,128)S(1)} %bitcast.60, f32[1024,1024]{1,0:T(8,128)} %copy-done), kind=kOutput, calls=%fused_computation.11 | convolution fusion | flops 12582912 | bytes 4202496 | tf_op jit(solution)/shard_map/dot_general | solution.py:68
  158.6 0.0 copy-start.1
  158.6 6.7 %all_to_all.51 = f32[4,1,1024]{2,1,0:T(1,128)S(1)} all-to-all(f32[4,1,1024]{2,1,0:T(1,128)S(1)} %broadcast_in_dim.30), channel_id=1, replica_groups=mesh['batch'=4,'proto'=64] {'batch'}, dimensions={0} | all-to-all | bytes 32768 | tf_op jit(solution)/shard_map/all_to_all | solution.py:24
  165.3 4.4 %fusion.4 = f32[1,1024]{1,0:T(1,128)S(1)} fusion(f32[1024,1]{0,1:T(1,128)S(1)} %bitcast.56, f32[1024,1024]{1,0:T(8,128)} %copy-done), kind=kOutput, calls=%fused_computation.8 | convolution fusion | flops 12582912 | bytes 4202496 | tf_op jit(solution)/shard_map/dot_general | solution.py:71
  169.8 0.8 broadcast_in_dim.31
  170.6 7.4 %all-to-all-start.6 = ((f32[64,1,1024]{2,1,0:T(1,128)}), f32[64,1,1024]{2,1,0:T(1,128)S(1)}, u32[]{:S(2)}, u32[]{:S(2)}) async-start(f32[64,1,1024]{2,1,0:T(1,128)} %broadcast_in_dim.31), calls=%async_computation.6 | async-start | bytes 524288 | tf_op jit(solution)/shard_map/all_to_all | solution.py:24
  178.0 0.0 all-gather.2.cloned.1.call-done
  178.0 2.1 multiply_reduce_fusion
  180.1 9.9 %all-to-all-done.6 = f32[64,1,1024]{2,1,0:T(1,128)S(1)} async-done(((f32[64,1,1024]{2,1,0:T(1,128)}), f32[64,1,1024]{2,1,0:T(1,128)S(1)}, u32[]{:S(2)}, u32[]{:S(2)}) %all-to-all-start.6) | async-done | bytes 262176 | tf_op jit(solution)/shard_map/all_to_all | solution.py:24
  190.0 0.2 reduce_sum.115
  190.2 0.0 copy-done.1
  190.2 6.9 %fusion.2 = (f32[1024]{0:T(1024)S(1)}, f32[1024]{0:T(1024)S(1)}, bf16[1024,1024]{0,1:T(8,128)(2,1)}) fusion(f32[1024]{0:T(1024)S(1)} %add_rsqrt_fusion, f32[1024]{0:T(1024)S(1)} %divide_multiply_fusion, f32[1024]{0:T(1024)S(1)} %multiply_divide_fusion, f32[1024,1024]{1,0:T(8,128)} %copy-done, bf16[1024,1024]{0,1:T(8,128)(2,1)} %all-gather.2.cloned.1.call-done, ...), kind=kOutput, calls=%fused_computation.6 | convolution fusion | flops 2160064512 | bytes 10510336 | tf_op jit(solution)/shard_map/dot_general | solution.py:48
  197.1 1.1 broadcast_in_dim.32
  198.2 6.0 %all-to-all-start.7 = ((f32[64,1,2048]{2,1,0:T(1,128)}), f32[64,1,2048]{2,1,0:T(1,128)S(1)}, u32[]{:S(2)}, u32[]{:S(2)}) async-start(f32[64,1,2048]{2,1,0:T(1,128)} %broadcast_in_dim.32), calls=%async_computation.7 | async-start | bytes 1048576 | tf_op jit(solution)/shard_map/all_to_all | solution.py:24
  204.2 3.9 %copy.16 = bf16[1024,1024]{1,0:T(8,128)(2,1)} copy(bf16[1024,1024]{0,1:T(8,128)(2,1)} %get-tuple-element.12) | data formatting | bytes 4194304
  208.2 13.3 %all-to-all-done.7 = f32[64,1,2048]{2,1,0:T(1,128)S(1)} async-done(((f32[64,1,2048]{2,1,0:T(1,128)}), f32[64,1,2048]{2,1,0:T(1,128)S(1)}, u32[]{:S(2)}, u32[]{:S(2)}) %all-to-all-start.7) | async-done | bytes 524320 | tf_op jit(solution)/shard_map/all_to_all | solution.py:24
  221.5 0.3 reduce_sum.119
  221.8 0.6 slice_subtract_fusion
  (16 shorter events, 0.2 us)
Async XLA Ops:
  9.5 65.5 %all-to-all-start = ((bf16[64,1024,16]{1,2,0:T(8,128)(2,1)}), bf16[64,1024,16]{1,2,0:T(8,128)(2,1)S(1)}, u32[]{:S(2)}, u32[]{:S(2)}) async-start(bf16[64,1024,16]{1,2,0:T(8,128)(2,1)} %stack.2), calls=%async_computation | async-start | bytes 4194304 | tf_op jit(solution)/shard_map/all_to_all | solution.py:14
  22.7 155.4 %all-gather.2.cloned.1.call-start = ((), (), s32[]{:S(2)}) async-start(), calls=%async_computation.8 | async-start | bytes 2129920 | tf_op jit(solution)/shard_map/all_gather | solution.py:58
  79.5 1.9 copy-start
  158.6 31.6 %copy-start.1 = (bf16[1024,1024]{1,0:T(8,128)(2,1)S(1)}, bf16[1024,1024]{1,0:T(8,128)(2,1)}, u32[]{:S(2)}) copy-start(bf16[1024,1024]{1,0:T(8,128)(2,1)} %param.5) | copy-start | bytes 6291460
  170.6 19.4 %all-to-all-start.6 = ((f32[64,1,1024]{2,1,0:T(1,128)}), f32[64,1,1024]{2,1,0:T(1,128)S(1)}, u32[]{:S(2)}, u32[]{:S(2)}) async-start(f32[64,1,1024]{2,1,0:T(1,128)} %broadcast_in_dim.31), calls=%async_computation.6 | async-start | bytes 524288 | tf_op jit(solution)/shard_map/all_to_all | solution.py:24
  198.2 23.3 %all-to-all-start.7 = ((f32[64,1,2048]{2,1,0:T(1,128)}), f32[64,1,2048]{2,1,0:T(1,128)S(1)}, u32[]{:S(2)}, u32[]{:S(2)}) async-start(f32[64,1,2048]{2,1,0:T(1,128)} %broadcast_in_dim.32), calls=%async_computation.7 | async-start | bytes 1048576 | tf_op jit(solution)/shard_map/all_to_all | solution.py:24
Sparse Core Ops, SparseCore 0:
  26.2 81.1 all-gather.1
